TPU v7x, 32 devices: a whole 2x2x4 slice. The times are simulated.
32 devices in a mesh: kpt: 2 (over y), row: 4 (over x, core), col: 4 (over z).
Axes of the slice: x: 2, y: 2, z: 4, core: 2. Of those that a mesh axis runs over, the one named last changes fastest.
Arguments:
- left_blocks: bfloat16 [8, 64, 2, 2, 128, 128], P(('kpt', 'row'), 'col'), parts along dimension 0, may hold values from -0.5 to 0.5
- left_rows: int32 [8, 64, 2], P(('kpt', 'row'), 'col'), parts along dimension 0, may hold values from 0 to 7, as said below
- left_count: int32 [8, 64], P(('kpt', 'row'), 'col'), parts along dimension 0, may hold values from 1 to 2, as said below
- left_level: int32 [8, 64, 2], P(('kpt', 'row'), 'col'), parts along dimension 0, may hold values from 0 to 7
- right_blocks: bfloat16 [2, 64, 4, 4, 2, 128, 128], P('kpt', 'row', 'col'), parts along dimension 0, may hold values from -6 to 6
- right_cols: int32 [2, 64, 4, 4], P('kpt', 'row', 'col'), parts along dimension 0, may hold values from 0 to 15, as said below
- right_count: int32 [2, 64, 4], P('kpt', 'row', 'col'), parts along dimension 0, may hold values from 1 to 4, as said below
- right_level: int32 [2, 64, 4, 4], P('kpt', 'row', 'col'), parts along dimension 0, may hold values from 0 to 7
Outputs:
- product_blocks: bfloat16 [64, 64, 2, 128, 128], P(('kpt', 'row'), 'col'), parts along dimension 0
There are 2 independent parts, one for each index of `kpt`. A program takes and returns all parts, laid end to end along the dimension named above; each array names one. Nothing has to cross between parts.
Inputs may be any that keep to these rules, and one draw needn't show every extreme that they name: `left_rows`: the 2 slots of one row group and block column name distinct block rows. `left_count`: in every row group some block column has all 2 slots live. `right_cols`: the 4 slots of one block row and column group name distinct block columns. `right_count`: in every column group some block row has all 4 slots live.
All inputs are finite; a program needn't handle non-finite values.
Results may differ from a plain program's by a relative error of at most 0.001.
Values may be sent and summed in bfloat16 or wider, within the bound.
A program may use at most 256 MiB of HBM per device.

v0:
```python
import jax
import jax.numpy as jnp
from jax import lax
from jax.sharding import PartitionSpec as P

GR = 8
LEVEL_CUT = 7


def pair_products(left_pack, right_pack, total):
    left_blocks, left_rows, left_count, left_level = left_pack
    right_blocks, right_cols, right_count, right_level = right_pack
    slots_left = left_rows.shape[1]
    slots_right = right_cols.shape[1]
    live_left = jnp.arange(slots_left, dtype=jnp.int32)[None, :] < left_count[:, None]
    live_right = jnp.arange(slots_right, dtype=jnp.int32)[None, :] < right_count[:, None]
    kept = live_left[:, :, None] & live_right[:, None, :]
    kept = kept & (left_level[:, :, None] + right_level[:, None, :] >= LEVEL_CUT)
    terms = jnp.einsum(
        "kmcij,kndjl->kmncdil", left_blocks, right_blocks, preferred_element_type=jnp.float32
    )
    real_part = terms[:, :, :, 0, 0] - terms[:, :, :, 1, 1]
    imag_part = terms[:, :, :, 0, 1] + terms[:, :, :, 1, 0]
    product = jnp.stack([real_part, imag_part], axis=3) * kept[:, :, :, None, None, None].astype(
        jnp.float32
    )
    row_index = jnp.broadcast_to(left_rows[:, :, None], kept.shape).reshape(-1)
    col_index = jnp.broadcast_to(right_cols[:, None, :], kept.shape).reshape(-1)
    width = left_blocks.shape[-1]
    return total.at[row_index, col_index].add(product.reshape(-1, 2, width, width))


def body(
    left_blocks,
    left_rows,
    left_count,
    left_level,
    right_blocks,
    right_cols,
    right_count,
    right_level,
):
    left_pack = (left_blocks[0], left_rows[0], left_count[0], left_level[0])
    right_pack = (
        right_blocks[:, :, 0],
        right_cols[:, :, 0],
        right_count[:, :, 0],
        right_level[:, :, 0],
    )
    width = left_blocks.shape[-1]
    panel_rows = left_blocks.shape[1]
    total = jnp.zeros((GR, panel_rows, 2, width, width), jnp.float32)
    whole = (
        lax.all_gather(right_pack[0], "row", axis=1, tiled=True),
        lax.all_gather(right_pack[1], "row", axis=1, tiled=True),
        lax.all_gather(right_pack[2], "row", axis=1, tiled=True),
        lax.all_gather(right_pack[3], "row", axis=1, tiled=True),
    )
    merged = whole[0].shape[0] * whole[0].shape[1]
    flat = jax.tree.map(lambda member: member.reshape((merged,) + member.shape[2:]), whole)
    carry = total
    piece = (
        lax.all_gather(left_pack[0], "col", axis=0, tiled=True),
        lax.all_gather(left_pack[1], "col", axis=0, tiled=True),
        lax.all_gather(left_pack[2], "col", axis=0, tiled=True),
        lax.all_gather(left_pack[3], "col", axis=0, tiled=True),
    )
    count = piece[0].shape[0]
    for first in range(0, count, panel_rows):
        size = min(panel_rows, count - first)
        left_part = jax.tree.map(lambda member: member[first : first + size], piece)
        right_part = jax.tree.map(
            lambda member: lax.dynamic_slice_in_dim(member, first, size, 0), flat
        )
        carry = pair_products(left_part, right_part, carry)
    total = carry
    return total.astype(jnp.bfloat16)


def solution(mesh):
    in_specs = (
        P(("kpt", "row"), "col", None, None, None, None),
        P(("kpt", "row"), "col", None),
        P(("kpt", "row"), "col"),
        P(("kpt", "row"), "col", None),
        P("kpt", "row", "col", None, None, None, None),
        P("kpt", "row", "col", None),
        P("kpt", "row", "col"),
        P("kpt", "row", "col", None),
    )
    out_specs = P(("kpt", "row"), "col", None, None, None)
    return jax.shard_map(body, mesh=mesh, in_specs=in_specs, out_specs=out_specs, check_vma=False)
```

profile of v0, /device:TPU:0, one launch (start us, length us, event | category | flops | bytes accessed | tf_op | source)
XLA Modules:
  0.0 728.9 jit_solution(17531730856529968428)
XLA Ops:
  13.2 14.8 %all-gather.6 = s32[1,64,2]{2,0,1:T(1,128)S(1)} all-gather(s32[1,16,2]{2,0,1:T(1,128)S(1)} %copy.67), channel_id=8, replica_groups=mesh['kpt'=2,'row'=4,'col'=4] {'col'}, dimensions={1}, use_global_device_ids=true | all-gather | bytes 640 | tf_op jit(solution)/shard_map/all_gather | solution.py:66
  49.2 13.1 %all-gather = s32[1,64,2]{2,0,1:T(1,128)S(1)} all-gather(s32[1,16,2]{2,0,1:T(1,128)S(1)} %copy.55), channel_id=2, replica_groups=mesh['kpt'=2,'row'=4,'col'=4] {'col'}, dimensions={1}, use_global_device_ids=true | all-gather | bytes 640 | tf_op jit(solution)/shard_map/all_gather | solution.py:64
  74.0 43.9 %all-gather.11.cloned.1.call-done = bf16[1,64,1,4,2,128,128]{6,5,4,3,2,0,1:T(8,128)(2,1)} async-done(((bf16[1,16,1,4,2,128,128]{6,5,4,3,2,0,1:T(8,128)(2,1)}), bf16[1,64,1,4,2,128,128]{6,5,4,3,2,0,1:T(8,128)(2,1)}) %all-gather.11.cloned.1.call-update) | async-done | bytes 16777232 | tf_op jit(solution)/shard_map/all_gather | solution.py:54
  118.0 22.4 %copy.62 = bf16[1,64,1,4,2,128,128]{5,6,4,3,1,2,0:T(8,128)(2,1)} copy(bf16[1,64,1,4,2,128,128]{6,5,4,3,2,0,1:T(8,128)(2,1)} %all-gather.11.cloned.1.call-done) | data formatting | bytes 33554432 | tf_op jit(solution)/shard_map/all_gather | solution.py:54
  140.3 128.9 %all-gather.13.cloned.1.call-done = bf16[1,64,2,2,128,128]{5,4,3,2,0,1:T(8,128)(2,1)} async-done(((bf16[1,16,2,2,128,128]{5,4,3,2,0,1:T(8,128)(2,1)}), bf16[1,64,2,2,128,128]{5,4,3,2,0,1:T(8,128)(2,1)}) %all-gather.13.cloned.1.call-update) | async-done | bytes 8388624 | tf_op jit(solution)/shard_map/all_gather | solution.py:63
  269.2 18.5 %convolution_bitcast_fusion.3 = f32[16,2,4,2,2,128,128]{5,6,3,1,4,2,0:T(8,128)} fusion(bf16[1,64,4,2,128,128]{4,5,3,2,1,0:T(8,128)(2,1)} %bitcast.137, bf16[1,64,2,2,128,128]{5,4,3,2,1,0:T(8,128)(2,1)} %bitcast.149), kind=kOutput, calls=%fused_computation.11 | convolution fusion | flops 2147483648 | bytes 39845888 | tf_op jit(solution)/shard_map/kmcij,kndjl->kmncdil/dot_general | solution.py:19
  287.7 18.5 %convolution_bitcast_fusion.2 = f32[16,2,4,2,2,128,128]{5,6,3,1,4,2,0:T(8,128)} fusion(bf16[1,64,4,2,128,128]{4,5,3,2,1,0:T(8,128)(2,1)} %bitcast.138, bf16[1,64,2,2,128,128]{5,4,3,2,1,0:T(8,128)(2,1)} %bitcast.150), kind=kOutput, calls=%fused_computation.10 | convolution fusion | flops 2147483648 | bytes 39845888 | tf_op jit(solution)/shard_map/kmcij,kndjl->kmncdil/dot_general | solution.py:19
  306.1 18.7 %convolution_bitcast_fusion.1 = f32[16,2,4,2,2,128,128]{5,6,3,1,4,2,0:T(8,128)} fusion(bf16[1,64,4,2,128,128]{4,5,3,2,1,0:T(8,128)(2,1)} %bitcast.139, bf16[1,64,2,2,128,128]{5,4,3,2,1,0:T(8,128)(2,1)} %bitcast.151), kind=kOutput, calls=%fused_computation.9 | convolution fusion | flops 2147483648 | bytes 39845888 | tf_op jit(solution)/shard_map/kmcij,kndjl->kmncdil/dot_general | solution.py:19
  324.8 18.5 %convolution_bitcast_fusion = f32[16,2,4,2,2,128,128]{5,6,3,1,4,2,0:T(8,128)} fusion(bf16[1,64,4,2,128,128]{4,5,3,2,1,0:T(8,128)(2,1)} %bitcast.140, bf16[1,64,2,2,128,128]{5,4,3,2,1,0:T(8,128)(2,1)} %bitcast.152), kind=kOutput, calls=%fused_computation.8 | convolution fusion | flops 2147483648 | bytes 39845888 | tf_op jit(solution)/shard_map/kmcij,kndjl->kmncdil/dot_general | solution.py:19
  343.3 19.3 %slice_subtract_fusion.3 = (f32[16,2,4,1,1,128,128]{5,6,3,1,4,2,0:T(8,128)}, f32[16,2,4,1,1,128,128]{5,6,3,1,4,2,0:T(8,128)}) fusion(f32[16,2,4,2,2,128,128]{5,6,3,1,4,2,0:T(8,128)} %convolution_bitcast_fusion.3), kind=kLoop, calls=%fused_computation.19 | loop fusion | flops 4194304 | bytes 50331648 | tf_op jit(solution)/shard_map/sub | solution.py:22
  362.6 9.3 %copy.65 = f32[16,2,4,1,1,128,128]{6,5,2,1,0,4,3:T(8,128)} copy(f32[16,2,4,1,1,128,128]{5,6,3,1,4,2,0:T(8,128)} %get-tuple-element.11) | data formatting | bytes 16777216 | tf_op jit(solution)/shard_map/sub | solution.py:22
  371.9 9.2 %copy.66 = f32[16,2,4,1,1,128,128]{6,5,2,1,0,4,3:T(8,128)} copy(f32[16,2,4,1,1,128,128]{5,6,3,1,4,2,0:T(8,128)} %get-tuple-element.12) | data formatting | bytes 16777216 | tf_op jit(solution)/shard_map/add | solution.py:23
  394.0 19.4 %slice_subtract_fusion.2 = (f32[16,2,4,1,1,128,128]{5,6,3,1,4,2,0:T(8,128)}, f32[16,2,4,1,1,128,128]{5,6,3,1,4,2,0:T(8,128)}) fusion(f32[16,2,4,2,2,128,128]{5,6,3,1,4,2,0:T(8,128)} %convolution_bitcast_fusion.2), kind=kLoop, calls=%fused_computation.17 | loop fusion | flops 4194304 | bytes 50331648 | tf_op jit(solution)/shard_map/sub | solution.py:22
  413.3 9.7 %copy.79 = f32[16,2,4,1,1,128,128]{6,5,2,1,0,4,3:T(8,128)} copy(f32[16,2,4,1,1,128,128]{5,6,3,1,4,2,0:T(8,128)} %get-tuple-element.9) | data formatting | bytes 16777216 | tf_op jit(solution)/shard_map/sub | solution.py:22
  423.0 9.2 %copy.80 = f32[16,2,4,1,1,128,128]{6,5,2,1,0,4,3:T(8,128)} copy(f32[16,2,4,1,1,128,128]{5,6,3,1,4,2,0:T(8,128)} %get-tuple-element.10) | data formatting | bytes 16777216 | tf_op jit(solution)/shard_map/add | solution.py:23
  445.1 19.3 %slice_subtract_fusion.1 = (f32[16,2,4,1,1,128,128]{5,6,3,1,4,2,0:T(8,128)}, f32[16,2,4,1,1,128,128]{5,6,3,1,4,2,0:T(8,128)}) fusion(f32[16,2,4,2,2,128,128]{5,6,3,1,4,2,0:T(8,128)} %convolution_bitcast_fusion.1), kind=kLoop, calls=%fused_computation.15 | loop fusion | flops 4194304 | bytes 50331648 | tf_op jit(solution)/shard_map/sub | solution.py:22
  464.4 9.2 %copy.91 = f32[16,2,4,1,1,128,128]{6,5,2,1,0,4,3:T(8,128)} copy(f32[16,2,4,1,1,128,128]{5,6,3,1,4,2,0:T(8,128)} %get-tuple-element.7) | data formatting | bytes 16777216 | tf_op jit(solution)/shard_map/sub | solution.py:22
  473.7 9.2 %copy.92 = f32[16,2,4,1,1,128,128]{6,5,2,1,0,4,3:T(8,128)} copy(f32[16,2,4,1,1,128,128]{5,6,3,1,4,2,0:T(8,128)} %get-tuple-element.8) | data formatting | bytes 16777216 | tf_op jit(solution)/shard_map/add | solution.py:23
  495.8 19.3 %slice_subtract_fusion = (f32[16,2,4,1,1,128,128]{5,6,3,1,4,2,0:T(8,128)}, f32[16,2,4,1,1,128,128]{5,6,3,1,4,2,0:T(8,128)}) fusion(f32[16,2,4,2,2,128,128]{5,6,3,1,4,2,0:T(8,128)} %convolution_bitcast_fusion), kind=kLoop, calls=%fused_computation.13 | loop fusion | flops 4194304 | bytes 50331648 | tf_op jit(solution)/shard_map/sub | solution.py:22
  524.4 9.2 %copy.104 = f32[16,2,4,1,1,128,128]{6,5,2,1,0,4,3:T(8,128)} copy(f32[16,2,4,1,1,128,128]{5,6,3,1,4,2,0:T(8,128)} %get-tuple-element.6) | data formatting | bytes 16777216 | tf_op jit(solution)/shard_map/add | solution.py:23
  554.3 39.5 %scatter_fusion = f32[8,16,2,128,128]{4,3,2,1,0:T(8,128)} fusion(f32[8,16,2,128,128]{4,3,2,1,0:T(8,128)} %broadcast_in_dim.26, s32[128]{0:T(128)S(1)} %copy-done.3, f32[128,2,128,128]{3,2,1,0:T(8,128)} %copy.73), kind=kCustom, calls=%fused_computation | custom fusion | flops 4194304 | bytes 50332672 | tf_op jit(solution)/shard_map/scatter-add | solution.py:30
  593.8 39.8 %scatter_fusion.1 = f32[8,16,2,128,128]{4,3,2,1,0:T(8,128)} fusion(f32[8,16,2,128,128]{4,3,2,1,0:T(8,128)} %scatter_fusion, s32[128]{0:T(128)S(1)} %copy-done.2, f32[128,2,128,128]{3,2,1,0:T(8,128)} %copy.85), kind=kCustom, calls=%fused_computation.1 | custom fusion | flops 4194304 | bytes 50332672 | tf_op jit(solution)/shard_map/scatter-add | solution.py:30
  633.6 39.4 %scatter_fusion.2 = f32[8,16,2,128,128]{4,3,2,1,0:T(8,128)} fusion(f32[8,16,2,128,128]{4,3,2,1,0:T(8,128)} %scatter_fusion.1, s32[128]{0:T(128)S(1)} %copy-done.1, f32[128,2,128,128]{3,2,1,0:T(8,128)} %copy.97), kind=kCustom, calls=%fused_computation.2 | custom fusion | flops 4194304 | bytes 50332672 | tf_op jit(solution)/shard_map/scatter-add | solution.py:30
  673.0 39.7 %scatter_fusion.3 = f32[8,16,2,128,128]{4,3,2,1,0:T(8,128)} fusion(f32[8,16,2,128,128]{4,3,2,1,0:T(8,128)} %scatter_fusion.2, s32[128]{0:T(128)S(1)} %copy-done, f32[128,2,128,128]{3,2,1,0:T(8,128)} %copy.109), kind=kCustom, calls=%fused_computation.3 | custom fusion | flops 4194304 | bytes 50332672 | tf_op jit(solution)/shard_map/scatter-add | solution.py:30
  (79 shorter events, 115.9 us)
Async XLA Ops:
  6.5 111.4 %all-gather.11.cloned.1.call-start = ((), (), s32[]{:S(2)}) async-start(), calls=%async_computation | async-start | bytes 20971520 | tf_op jit(solution)/shard_map/all_gather | solution.py:54
  7.3 261.9 %all-gather.13.cloned.1.call-start = ((), (), s32[]{:S(2)}) async-start(), calls=%async_computation.1 | async-start | bytes 10485760 | tf_op jit(solution)/shard_map/all_gather | solution.py:63
  473.7 9.2 %copy-start.4 = (f32[128]{0:T(128)S(1)}, f32[128]{0:T(128)}, u32[]{:S(2)}) copy-start(f32[128]{0:T(128)} %reshape.718) | copy-start | bytes 1540
  524.4 9.2 %copy-start.5 = (f32[128]{0:T(128)S(1)}, f32[128]{0:T(128)}, u32[]{:S(2)}) copy-start(f32[128]{0:T(128)} %reshape.719) | copy-start | bytes 1540
  546.4 7.9 %copy-start.3 = (s32[128]{0:T(128)S(1)}, s32[128]{0:T(128)}, u32[]{:S(2)}) copy-start(s32[128]{0:T(128)} %fusion.4) | copy-start | bytes 1540
  554.3 39.5 %copy-start.2 = (s32[128]{0:T(128)S(1)}, s32[128]{0:T(128)}, u32[]{:S(2)}) copy-start(s32[128]{0:T(128)} %fusion.5) | copy-start | bytes 1540
  593.8 39.8 %copy-start.1 = (s32[128]{0:T(128)S(1)}, s32[128]{0:T(128)}, u32[]{:S(2)}) copy-start(s32[128]{0:T(128)} %fusion.6) | copy-start | bytes 1540
  633.6 39.4 %copy-start = (s32[128]{0:T(128)S(1)}, s32[128]{0:T(128)}, u32[]{:S(2)}) copy-start(s32[128]{0:T(128)} %fusion.7) | copy-start | bytes 1540
Sparse Core Ops, SparseCore 0:
  8.9 109.0 all-gather.10
  119.5 149.6 all-gather.12
where the time goes:
time: 734 us; the launch traced here: 729 us
  other arithmetic  275 us (37%)
  waiting for transfers between devices  174 us (24%)
  local copies, waits for them, and re-layouts  139 us (19%)
  matrix products  74.1 us (10%)
  blocking collectives  51.8 us (7%)
  between operations  14.9 us (2%)
    scatter-add x4, other arithmetic, pair_products(): total.at[row_index, col_index].add(product.reshape(-1, 2, width, width))  158 us
    all_gather x1, waiting for transfers between devices, body(): lax.all_gather(left_pack[0], 'col', axis=0, tiled=True)  129 us
    sub x4, other arithmetic, pair_products(): real_part = terms[:, :, :, 0, 0] - terms[:, :, :, 1, 1]  77.3 us
    dot_general x4, matrix products, pair_products(): jnp.einsum('kmcij,kndjl->kmncdil', left_blocks, right_blocks, preferred_e...  74.1 us
    all_gather x1, waiting for transfers between devices, body(): lax.all_gather(right_pack[0], 'row', axis=1, tiled=True)  43.9 us
    sub x4, local copies, waits for them, and re-layouts, pair_products(): real_part = terms[:, :, :, 0, 0] - terms[:, :, :, 1, 1]  37.4 us
    add x4, local copies, waits for them, and re-layouts, pair_products(): imag_part = terms[:, :, :, 0, 1] + terms[:, :, :, 1, 0]  37 us
    mul x4, other arithmetic, pair_products(): jnp.stack([real_part, imag_part], axis=3)  27.1 us
  transfers between devices with their start and end apart: 2, of which 2 were waited for; matrix products, arithmetic and copies ran while one was open for 5% of the time, Pallas kernels for 0%

commit v1 on v0

v1 whole, which is shorter than its diff:
```python
import functools

import jax
import jax.numpy as jnp
from jax import lax
from jax.experimental import pallas as pl
from jax.experimental.pallas import tpu as pltpu
from jax.sharding import PartitionSpec as P

GR = 8
LEVEL_CUT = 7
DEAD = -1000
UNROLL = 4
LEFT_CUTS = 2
RIGHT_CUTS = 4
MESH = pl.DeviceIdType.MESH


def gather_kernel(
    n_row, n_col, left, right, left_meta, right_meta,
    left_all, right_all, left_meta_all, right_meta_all,
    up_send, up_recv, down_send, down_recv,
    x_send, x_recv, own_send, own_recv, pass_send, pass_recv,
    lm_send, lm_recv, rm_send, rm_recv,
):
    row = lax.axis_index("row")
    col = lax.axis_index("col")
    n_chip = n_row // 2
    chip, core = row // 2, row % 2
    partner = chip * 2 + 1 - core

    barrier = pltpu.get_barrier_semaphore()
    for step in range(1, n_row):
        pl.semaphore_signal(
            barrier, inc=1, device_id={"row": (row + step) % n_row}, device_id_type=MESH
        )
    for step in range(1, n_col):
        pl.semaphore_signal(
            barrier, inc=1, device_id={"col": (col + step) % n_col}, device_id_type=MESH
        )
    pl.semaphore_wait(barrier, n_row + n_col - 2)

    left_size = left.shape[0] // LEFT_CUTS
    right_size = right.shape[1] // RIGHT_CUTS

    def left_copy(step, cut, up):
        panel = col - step if up else col + step
        span = pl.ds(cut * left_size, left_size)
        source = left.at[span] if step == 0 else left_all.at[panel, span]
        send, recv = (up_send, up_recv) if up else (down_send, down_recv)
        return pltpu.make_async_remote_copy(
            src_ref=source, dst_ref=left_all.at[panel, span],
            send_sem=send.at[step, cut], recv_sem=recv.at[step, cut],
            device_id={"col": col + 1 if up else col - 1}, device_id_type=MESH,
        )

    def left_sends(step, up):
        if up:
            return (col + 1 < n_col) & (col - step >= 0)
        return (col - 1 >= 0) & (col + step < n_col)

    def left_receives(step, up):
        return col - 1 - step >= 0 if up else col + 1 + step < n_col

    def across(step, cut):
        span = pl.ds(cut * right_size, right_size)
        other = ((chip + step) % n_chip) * 2 + core
        return pltpu.make_async_remote_copy(
            src_ref=right.at[:, span], dst_ref=right_all.at[:, row, span],
            send_sem=x_send.at[step - 1, cut], recv_sem=x_recv.at[step - 1, cut],
            device_id={"row": other}, device_id_type=MESH,
        )

    def passed(step, cut):
        span = pl.ds(cut * right_size, right_size)
        panel = ((chip + n_chip - step) % n_chip) * 2 + core
        return pltpu.make_async_remote_copy(
            src_ref=right_all.at[:, panel, span], dst_ref=right_all.at[:, panel, span],
            send_sem=pass_send.at[step - 1, cut], recv_sem=pass_recv.at[step - 1, cut],
            device_id={"row": partner}, device_id_type=MESH,
        )

    own = pltpu.make_async_remote_copy(
        src_ref=right, dst_ref=right_all.at[:, row],
        send_sem=own_send, recv_sem=own_recv,
        device_id={"row": partner}, device_id_type=MESH,
    )

    def meta_copies():
        for step in range(1, n_col):
            yield pltpu.make_async_remote_copy(
                src_ref=left_meta, dst_ref=left_meta_all.at[col],
                send_sem=lm_send.at[step - 1], recv_sem=lm_recv.at[step - 1],
                device_id={"col": (col + step) % n_col}, device_id_type=MESH,
            )
        for step in range(1, n_row):
            yield pltpu.make_async_remote_copy(
                src_ref=right_meta, dst_ref=right_meta_all.at[row],
                send_sem=rm_send.at[step - 1], recv_sem=rm_recv.at[step - 1],
                device_id={"row": (row + step) % n_row}, device_id_type=MESH,
            )

    for copy in meta_copies():
        copy.start()
    for cut in range(LEFT_CUTS):
        for up in (True, False):
            pl.when(left_sends(0, up))(left_copy(0, cut, up).start)
    for step in range(1, n_chip):
        for cut in range(RIGHT_CUTS):
            across(step, cut).start()
    own.start()
    left_meta_all[col] = left_meta[...]
    right_meta_all[row] = right_meta[...]

    def take_left(step, cut):
        for up in (True, False):
            pl.when(left_receives(step, up))(left_copy(step, cut, up).wait_recv)
            if step + 1 < n_col - 1:
                pl.when(left_sends(step + 1, up))(left_copy(step + 1, cut, up).start)

    def take_right(step, cut):
        across(step, cut).wait_recv()
        passed(step, cut).start()

    left_jobs = [
        ((step * LEFT_CUTS + cut + 1) / LEFT_CUTS, functools.partial(take_left, step, cut))
        for step in range(n_col - 1) for cut in range(LEFT_CUTS)
    ]
    right_jobs = [
        (2 * ((step - 1) * RIGHT_CUTS + cut + 1) / RIGHT_CUTS + 0.1,
         functools.partial(take_right, step, cut))
        for step in range(1, n_chip) for cut in range(RIGHT_CUTS)
    ]
    for _, job in sorted(left_jobs + right_jobs, key=lambda entry: entry[0]):
        job()

    own.wait()
    for step in range(1, n_chip):
        for cut in range(RIGHT_CUTS):
            across(step, cut).wait_send()
            passed(step, cut).wait()
    for step in range(n_col - 1):
        for cut in range(LEFT_CUTS):
            for up in (True, False):
                pl.when(left_sends(step, up))(left_copy(step, cut, up).wait_send)
    for copy in meta_copies():
        copy.wait()


def product_kernel(
    sizes, left, right, left_all, right_all, left_meta, right_meta,
    out, left_buf, right_buf, total, stage, pairs, counts, touched,
    left_sem, right_sem, out_sem,
):
    n_row, n_col, sets, per, ma, mb, kb_cols = sizes
    row = lax.axis_index("row")
    col = lax.axis_index("col")
    blocks = GR * kb_cols
    room = per * ma * mb + UNROLL

    def left_copy(panel, source):
        return pltpu.make_async_copy(source, left_buf.at[panel], left_sem.at[panel])

    def right_copy(panel, source):
        return pltpu.make_async_copy(source, right_buf.at[panel], right_sem.at[panel])

    for panel in range(n_col):
        which, at = panel // n_row, panel % n_row
        pl.when(col == panel)(left_copy(panel, left).start)
        pl.when(col != panel)(left_copy(panel, left_all.at[panel]).start)
        pl.when(row == at)(right_copy(panel, right.at[which]).start)
        pl.when(row != at)(right_copy(panel, right_all.at[which, at]).start)

    @pl.loop(0, blocks + 1)
    def _(block):
        touched[block] = 0

    for panel in range(n_col):
        which, at = panel // n_row, panel % n_row
        base = panel * room

        def gather(k, count):
            rights = []
            for n in range(mb):
                slot = (which * per + k) * mb + n
                rights.append((right_meta[at, 0, slot], right_meta[at, 1, slot]))
            for m in range(ma):
                slot = k * ma + m
                target = left_meta[panel, 0, slot] * kb_cols
                level = left_meta[panel, 1, slot]
                for n in range(mb):
                    code = slot * 1024 + k * mb + n
                    pairs[base + count] = code * 1024 + target + rights[n][0]
                    count = count + jnp.where(level + rights[n][1] >= LEVEL_CUT, 1, 0)
            return count

        count = lax.fori_loop(0, per, gather, jnp.int32(0))
        for extra in range(UNROLL):
            pairs[base + count + extra] = blocks
        counts[panel] = (count + UNROLL - 1) // UNROLL

    for panel in range(n_col):
        left_copy(panel, left).wait()
        right_copy(panel, right.at[0]).wait()

        @pl.loop(0, counts[panel])
        def _(group):
            done = []
            for lane in range(UNROLL):
                code = pairs[panel * room + group * UNROLL + lane]
                target = code & 1023
                block = left_buf[panel, code >> 20]
                width = block.shape[1]
                real, imag = block[:width], block[width:]
                matrix = jnp.concatenate(
                    [jnp.concatenate([real, -imag], axis=1), jnp.concatenate([imag, real], axis=1)],
                    axis=0,
                )
                other = right_buf[panel, (code >> 10) & 1023]
                done.append((target, jnp.dot(matrix, other, preferred_element_type=jnp.float32)))
            for target, product in done:
                old = touched[target] > 0
                total[target] = jnp.where(old, total[target], 0.0) + product
                touched[target] = 1

    def out_copy(line):
        span = pl.ds(line * kb_cols, kb_cols)
        return pltpu.make_async_copy(stage.at[span], out.at[span], out_sem.at[line])

    @pl.loop(0, GR)
    def _(line):
        @pl.loop(0, kb_cols, unroll=2)
        def _(k):
            block = line * kb_cols + k
            stage[block] = jnp.where(touched[block] > 0, total[block], 0.0).astype(stage.dtype)

        out_copy(line).start()

    @pl.loop(0, GR)
    def _(line):
        out_copy(line).wait()


def pack_meta(index, count, level):
    slots = index.shape[-1]
    live = jnp.arange(slots, dtype=jnp.int32) < count[..., None]
    level = jnp.where(live, level, DEAD)
    meta = jnp.stack([index.reshape(-1), level.reshape(-1)])
    width = -(-meta.shape[1] // 128) * 128
    return jnp.pad(meta, ((0, 6), (0, width - meta.shape[1])))


def body(
    n_row, n_col, left_blocks, left_rows, left_count, left_level,
    right_blocks, right_cols, right_count, right_level,
):
    _, per, ma, _, width, _ = left_blocks.shape
    sets, right_per, _, mb = right_blocks.shape[:4]
    assert right_per == per and sets * n_row == n_col and n_row % 2 == 0
    left = left_blocks.reshape(per * ma, 2 * width, width)
    right = right_blocks.reshape(sets, per * mb, 2 * width, width)
    left_meta = pack_meta(left_rows[0], left_count[0], left_level[0])
    right_meta = pack_meta(right_cols[:, :, 0], right_count[:, :, 0], right_level[:, :, 0])
    any_space = pl.BlockSpec(memory_space=pl.ANY)
    vmem = pl.BlockSpec(memory_space=pltpu.VMEM)
    smem = pl.BlockSpec(memory_space=pltpu.SMEM)
    dma = pltpu.SemaphoreType.DMA
    n_chip = n_row // 2
    left_shape = (n_col,) + left.shape
    right_shape = (sets, n_row) + right.shape[1:]
    gathered = pl.pallas_call(
        functools.partial(gather_kernel, n_row, n_col),
        out_shape=(
            jax.ShapeDtypeStruct(left_shape, left.dtype),
            jax.ShapeDtypeStruct(right_shape, right.dtype),
            jax.ShapeDtypeStruct((n_col,) + left_meta.shape, jnp.int32),
            jax.ShapeDtypeStruct((n_row,) + right_meta.shape, jnp.int32),
        ),
        in_specs=[any_space, any_space, vmem, vmem],
        out_specs=(any_space, any_space, vmem, vmem),
        scratch_shapes=[
            *[dma((n_col - 1, LEFT_CUTS))] * 4,
            *[dma((n_chip - 1, RIGHT_CUTS))] * 2,
            *[dma] * 2,
            *[dma((n_chip - 1, RIGHT_CUTS))] * 2,
            *[dma((n_col - 1,))] * 2,
            *[dma((n_row - 1,))] * 2,
        ],
        compiler_params=pltpu.CompilerParams(collective_id=0, has_side_effects=True),
        name="gather_panels",
    )(left, right, left_meta, right_meta)
    left_all, right_all, left_meta_all, right_meta_all = gathered
    kb_cols = n_row * sets * per // n_col
    blocks = GR * kb_cols
    room = per * ma * mb + UNROLL
    out = pl.pallas_call(
        functools.partial(product_kernel, (n_row, n_col, sets, per, ma, mb, kb_cols)),
        out_shape=jax.ShapeDtypeStruct((blocks, 2 * width, width), jnp.bfloat16),
        in_specs=[any_space] * 4 + [smem] * 2,
        out_specs=any_space,
        scratch_shapes=[
            pltpu.VMEM((n_col, per * ma, 2 * width, width), left.dtype),
            pltpu.VMEM((n_col, per * mb, 2 * width, width), right.dtype),
            pltpu.VMEM((blocks + 1, 2 * width, width), jnp.float32),
            pltpu.VMEM((blocks, 2 * width, width), jnp.bfloat16),
            pltpu.SMEM((n_col * room,), jnp.int32),
            pltpu.SMEM((n_col,), jnp.int32),
            pltpu.SMEM((blocks + 1,), jnp.int32),
            dma((n_col,)),
            dma((n_col,)),
            dma((GR,)),
        ],
        compiler_params=pltpu.CompilerParams(vmem_limit_bytes=60 * 1024 * 1024),
        name="pair_products",
    )(left, right, left_all, right_all, left_meta_all, right_meta_all)
    return out.reshape(GR, kb_cols, 2, width, width)


def solution(mesh):
    in_specs = (
        P(("kpt", "row"), "col", None, None, None, None),
        P(("kpt", "row"), "col", None),
        P(("kpt", "row"), "col"),
        P(("kpt", "row"), "col", None),
        P("kpt", "row", "col", None, None, None, None),
        P("kpt", "row", "col", None),
        P("kpt", "row", "col"),
        P("kpt", "row", "col", None),
    )
    out_specs = P(("kpt", "row"), "col", None, None, None)
    return jax.shard_map(
        functools.partial(body, mesh.shape["row"], mesh.shape["col"]),
        mesh=mesh, in_specs=in_specs, out_specs=out_specs, check_vma=False,
    )
```

time: 734 us -> 171 us (0.23)
  other arithmetic: 275 us -> 0.76 us
  waiting for transfers between devices: 174 us -> 0 us
  Pallas kernels: 0 us -> 163 us
  local copies, waits for them, and re-layouts: 139 us -> 5.58 us
  matrix products: 74.1 us -> 0 us
  blocking collectives: 51.8 us -> 0 us
  between operations: 14.9 us -> 0.07 us
    all_gather x2 -> x0, waiting for transfers between devices: 173 us -> none  [the longest x1 129 us: body(): lax.all_gather(left_pack[0], 'col', axis=0, tiled=True)]
    pallas_call x0 -> x2, Pallas kernels: none -> 163 us  [the longest x1 143 us: body(): pl.pallas_call(functools.partial(gather_kernel, n_row, n_col), out_shape=...]
    scatter-add x4 -> x0, other arithmetic: 158 us -> none  [pair_products(): total.at[row_index, col_index].add(product.reshape(-1, 2, width, width))]
    sub x4 -> x0, other arithmetic: 77.3 us -> none  [pair_products(): real_part = terms[:, :, :, 0, 0] - terms[:, :, :, 1, 1]]
    dot_general x4 -> x0, matrix products: 74.1 us -> none  [pair_products(): jnp.einsum('kmcij,kndjl->kmncdil', left_blocks, right_blocks, preferred_e...]
    all_gather x4 -> x0, blocking collectives: 38.9 us -> none  [the longest x1 14.8 us: body(): lax.all_gather(left_pack[3], 'col', axis=0, tiled=True)]
    sub x4 -> x0, local copies, waits for them, and re-layouts: 37.4 us -> none  [pair_products(): real_part = terms[:, :, :, 0, 0] - terms[:, :, :, 1, 1]]
    add x5 -> x0, local copies, waits for them, and re-layouts: 37 us -> none  [the longest x4 37 us: pair_products(): imag_part = terms[:, :, :, 0, 1] + terms[:, :, :, 1, 0]]
  transfers between devices with their start and end apart: 2 -> 0, of which waited for: 2 -> 0; matrix products, arithmetic and copies ran while one was open for 5% -> 0% of each run, Pallas kernels for 0% -> 0%
where the time goes in v1:
time: 171 us; the launch traced here: 170 us
  Pallas kernels  163 us (95%)
  local copies, waits for them, and re-layouts  5.58 us (3%)
    pallas_call x1, Pallas kernels, body(): pl.pallas_call(functools.partial(gather_kernel, n_row, n_col), out_shape=...  143 us
    pallas_call x1, Pallas kernels, body(): pl.pallas_call(functools.partial(product_kernel, (n_row, n_col, sets, per...  19.8 us

profile of v1, /device:TPU:0, one launch (start us, length us, event | category | flops | bytes accessed | tf_op | source)
XLA Modules:
  0.0 169.5 jit_solution(2434895613353729705)
XLA Ops:
  0.0 0.7 iota_compare_fusion
  0.7 0.1 lt.55
  0.8 0.8 copy.13
  1.6 0.1 stack_reshape_squeeze.6
  1.7 0.8 copy.14
  2.4 0.1 squeeze.6
  2.6 0.6 pad.8.left_meta
  3.2 0.8 copy.15
  3.9 0.1 stack_reshape_squeeze.7
  4.0 0.7 lt.58
  4.7 0.1 lt.59
  4.8 0.8 copy.16
  5.6 0.1 squeeze.7
  5.7 0.1 lt.57
  5.8 0.6 pad.9.right_meta
  6.4 143.3 %gather_panels.1 = (bf16[4,32,256,128]{3,2,1,0:T(8,128)(2,1)}, bf16[1,4,64,256,128]{4,3,2,1,0:T(8,128)(2,1)}, s32[4,8,128]{2,1,0:T(8,128)}, s32[4,8,128]{2,1,0:T(8,128)}) custom-call(bf16[32,256,128]{2,1,0:T(8,128)(2,1)} %bitcast.17, bf16[1,64,256,128]{3,2,1,0:T(8,128)(2,1)} %bitcast.15, s32[8,128]{1,0:T(8,128)} %pad.8.left_meta, s32[8,128]{1,0:T(8,128)} %pad.9.right_meta), custom_call_target="tpu_custom_call" | custom-call | tf_op jit(solution)/shard_map/gather_panels/pallas_call | solution.py:271
  149.7 19.8 %pair_products.1 = bf16[128,256,128]{2,1,0:T(8,128)(2,1)} custom-call(bf16[32,256,128]{2,1,0:T(8,128)(2,1)} %bitcast.18, bf16[1,64,256,128]{3,2,1,0:T(8,128)(2,1)} %bitcast.16, bf16[4,32,256,128]{3,2,1,0:T(8,128)(2,1)} %get-tuple-element.9.left_all, bf16[1,4,64,256,128]{4,3,2,1,0:T(8,128)(2,1)} %get-tuple-element.10.right_all, ...), custom_call_target="tpu_custom_call" | custom-call | tf_op jit(solution)/shard_map/pair_products/pallas_call | solution.py:296
  (5 shorter events, 0.0 us)

commit v2 on v1

--- a/solution.py
+++ b/solution.py
@@ -10,18 +10,19 @@
 GR = 8
 LEVEL_CUT = 7
 DEAD = -1000
-UNROLL = 4
+UNROLL = 16
 LEFT_CUTS = 2
+VMEM_BYTES = 62 * 1024 * 1024
 RIGHT_CUTS = 4
 MESH = pl.DeviceIdType.MESH
 
 
 def gather_kernel(
-    n_row, n_col, left, right, left_meta, right_meta,
+    n_row, n_col, left, right, meta,
     left_all, right_all, left_meta_all, right_meta_all,
     up_send, up_recv, down_send, down_recv,
     x_send, x_recv, own_send, own_recv, pass_send, pass_recv,
-    lm_send, lm_recv, rm_send, rm_recv,
+    lm_send, lm_recv, rm_send, rm_recv, left_sem, right_sem,
 ):
     row = lax.axis_index("row")
     col = lax.axis_index("col")
@@ -89,13 +90,13 @@
     def meta_copies():
         for step in range(1, n_col):
             yield pltpu.make_async_remote_copy(
-                src_ref=left_meta, dst_ref=left_meta_all.at[col],
+                src_ref=meta, dst_ref=left_meta_all.at[col],
                 send_sem=lm_send.at[step - 1], recv_sem=lm_recv.at[step - 1],
                 device_id={"col": (col + step) % n_col}, device_id_type=MESH,
             )
         for step in range(1, n_row):
             yield pltpu.make_async_remote_copy(
-                src_ref=right_meta, dst_ref=right_meta_all.at[row],
+                src_ref=meta, dst_ref=right_meta_all.at[row],
                 send_sem=rm_send.at[step - 1], recv_sem=rm_recv.at[step - 1],
                 device_id={"row": (row + step) % n_row}, device_id_type=MESH,
             )
@@ -109,8 +110,14 @@
         for cut in range(RIGHT_CUTS):
             across(step, cut).start()
     own.start()
-    left_meta_all[col] = left_meta[...]
-    right_meta_all[row] = right_meta[...]
+    kept = (
+        pltpu.make_async_copy(left, left_all.at[col], left_sem),
+        pltpu.make_async_copy(right, right_all.at[:, row], right_sem),
+    )
+    for copy in kept:
+        copy.start()
+    left_meta_all[col] = meta[...]
+    right_meta_all[row] = meta[...]
 
     def take_left(step, cut):
         for up in (True, False):
@@ -135,6 +142,8 @@
         job()
 
     own.wait()
+    for copy in kept:
+        copy.wait()
     for step in range(1, n_chip):
         for cut in range(RIGHT_CUTS):
             across(step, cut).wait_send()
@@ -148,80 +157,63 @@
 
 
 def product_kernel(
-    sizes, left, right, left_all, right_all, left_meta, right_meta,
-    out, left_buf, right_buf, total, stage, pairs, counts, touched,
-    left_sem, right_sem, out_sem,
+    sizes, left, right, left_meta, right_meta, out, total, stage, pairs, touched, out_sem,
 ):
     n_row, n_col, sets, per, ma, mb, kb_cols = sizes
-    row = lax.axis_index("row")
-    col = lax.axis_index("col")
     blocks = GR * kb_cols
-    room = per * ma * mb + UNROLL
-
-    def left_copy(panel, source):
-        return pltpu.make_async_copy(source, left_buf.at[panel], left_sem.at[panel])
-
-    def right_copy(panel, source):
-        return pltpu.make_async_copy(source, right_buf.at[panel], right_sem.at[panel])
-
-    for panel in range(n_col):
-        which, at = panel // n_row, panel % n_row
-        pl.when(col == panel)(left_copy(panel, left).start)
-        pl.when(col != panel)(left_copy(panel, left_all.at[panel]).start)
-        pl.when(row == at)(right_copy(panel, right.at[which]).start)
-        pl.when(row != at)(right_copy(panel, right_all.at[which, at]).start)
+    tall = sets * per
 
     @pl.loop(0, blocks + 1)
     def _(block):
         touched[block] = 0
 
+    count = jnp.int32(0)
     for panel in range(n_col):
         which, at = panel // n_row, panel % n_row
-        base = panel * room
 
         def gather(k, count):
+            line = which * per + k
+            live = right_meta[at, tall + 1 + which, k]
             rights = []
             for n in range(mb):
-                slot = (which * per + k) * mb + n
-                rights.append((right_meta[at, 0, slot], right_meta[at, 1, slot]))
+                level = right_meta[at, line, 2 * ma + mb + n]
+                rights.append(
+                    (right_meta[at, line, 2 * ma + n], jnp.where(n < live, level, DEAD))
+                )
+            live = left_meta[panel, tall, k]
+            slot = panel * per + k
             for m in range(ma):
-                slot = k * ma + m
-                target = left_meta[panel, 0, slot] * kb_cols
-                level = left_meta[panel, 1, slot]
+                target = left_meta[panel, k, m] * kb_cols
+                level = jnp.where(m < live, left_meta[panel, k, ma + m], DEAD)
                 for n in range(mb):
-                    code = slot * 1024 + k * mb + n
-                    pairs[base + count] = code * 1024 + target + rights[n][0]
+                    code = (slot * ma + m) * 1024 + slot * mb + n
+                    pairs[count] = code * 1024 + target + rights[n][0]
                     count = count + jnp.where(level + rights[n][1] >= LEVEL_CUT, 1, 0)
             return count
 
-        count = lax.fori_loop(0, per, gather, jnp.int32(0))
-        for extra in range(UNROLL):
-            pairs[base + count + extra] = blocks
-        counts[panel] = (count + UNROLL - 1) // UNROLL
-
-    for panel in range(n_col):
-        left_copy(panel, left).wait()
-        right_copy(panel, right.at[0]).wait()
-
-        @pl.loop(0, counts[panel])
-        def _(group):
-            done = []
-            for lane in range(UNROLL):
-                code = pairs[panel * room + group * UNROLL + lane]
-                target = code & 1023
-                block = left_buf[panel, code >> 20]
-                width = block.shape[1]
-                real, imag = block[:width], block[width:]
-                matrix = jnp.concatenate(
-                    [jnp.concatenate([real, -imag], axis=1), jnp.concatenate([imag, real], axis=1)],
-                    axis=0,
-                )
-                other = right_buf[panel, (code >> 10) & 1023]
-                done.append((target, jnp.dot(matrix, other, preferred_element_type=jnp.float32)))
-            for target, product in done:
-                old = touched[target] > 0
-                total[target] = jnp.where(old, total[target], 0.0) + product
-                touched[target] = 1
+        count = lax.fori_loop(0, per, gather, count, unroll=4)
+    for extra in range(UNROLL):
+        pairs[count + extra] = blocks
+
+    @pl.loop(0, (count + UNROLL - 1) // UNROLL)
+    def _(group):
+        done = []
+        for lane in range(UNROLL):
+            code = pairs[group * UNROLL + lane]
+            target = code & 1023
+            block = left[code >> 20]
+            width = block.shape[1]
+            real, imag = block[:width], block[width:]
+            matrix = jnp.concatenate(
+                [jnp.concatenate([real, -imag], axis=1), jnp.concatenate([imag, real], axis=1)],
+                axis=0,
+            )
+            other = right[(code >> 10) & 1023]
+            done.append((target, jnp.dot(matrix, other, preferred_element_type=jnp.float32)))
+        for target, product in done:
+            old = touched[target] > 0
+            total[target] = jnp.where(old, total[target], 0.0) + product
+            touched[target] = 1
 
     def out_copy(line):
         span = pl.ds(line * kb_cols, kb_cols)
@@ -229,7 +221,7 @@
 
     @pl.loop(0, GR)
     def _(line):
-        @pl.loop(0, kb_cols, unroll=2)
+        @pl.loop(0, kb_cols, unroll=4)
         def _(k):
             block = line * kb_cols + k
             stage[block] = jnp.where(touched[block] > 0, total[block], 0.0).astype(stage.dtype)
@@ -241,13 +233,9 @@
         out_copy(line).wait()
 
 
-def pack_meta(index, count, level):
-    slots = index.shape[-1]
-    live = jnp.arange(slots, dtype=jnp.int32) < count[..., None]
-    level = jnp.where(live, level, DEAD)
-    meta = jnp.stack([index.reshape(-1), level.reshape(-1)])
-    width = -(-meta.shape[1] // 128) * 128
-    return jnp.pad(meta, ((0, 6), (0, width - meta.shape[1])))
+def place(array, top, lane, rows):
+    tall, wide = array.shape
+    return jnp.pad(array, ((top, rows - tall - top), (lane, 128 - lane - wide)))
 
 
 def body(
@@ -259,8 +247,17 @@
     assert right_per == per and sets * n_row == n_col and n_row % 2 == 0
     left = left_blocks.reshape(per * ma, 2 * width, width)
     right = right_blocks.reshape(sets, per * mb, 2 * width, width)
-    left_meta = pack_meta(left_rows[0], left_count[0], left_level[0])
-    right_meta = pack_meta(right_cols[:, :, 0], right_count[:, :, 0], right_level[:, :, 0])
+    tall = sets * per
+    rows = -(-(tall + 1 + sets) // 8) * 8
+    meta = (
+        place(jnp.concatenate([left_rows[0], left_level[0]], axis=1), 0, 0, rows)
+        + place(left_count, tall, 0, rows)
+        + place(
+            jnp.concatenate([right_cols, right_level], axis=3).reshape(tall, 2 * mb),
+            0, 2 * ma, rows,
+        )
+        + place(right_count.reshape(sets, per), tall + 1, 0, rows)
+    )
     any_space = pl.BlockSpec(memory_space=pl.ANY)
     vmem = pl.BlockSpec(memory_space=pltpu.VMEM)
     smem = pl.BlockSpec(memory_space=pltpu.SMEM)
@@ -268,16 +265,17 @@
     n_chip = n_row // 2
     left_shape = (n_col,) + left.shape
     right_shape = (sets, n_row) + right.shape[1:]
+    limit = VMEM_BYTES - (n_col * left.size + n_row * right.size) * left.dtype.itemsize
     gathered = pl.pallas_call(
         functools.partial(gather_kernel, n_row, n_col),
         out_shape=(
-            jax.ShapeDtypeStruct(left_shape, left.dtype),
-            jax.ShapeDtypeStruct(right_shape, right.dtype),
-            jax.ShapeDtypeStruct((n_col,) + left_meta.shape, jnp.int32),
-            jax.ShapeDtypeStruct((n_row,) + right_meta.shape, jnp.int32),
+            pltpu.VMEM(left_shape, left.dtype),
+            pltpu.VMEM(right_shape, right.dtype),
+            jax.ShapeDtypeStruct((n_col,) + meta.shape, jnp.int32),
+            jax.ShapeDtypeStruct((n_row,) + meta.shape, jnp.int32),
         ),
-        in_specs=[any_space, any_space, vmem, vmem],
-        out_specs=(any_space, any_space, vmem, vmem),
+        in_specs=[any_space, any_space, vmem],
+        out_specs=(vmem, vmem, vmem, vmem),
         scratch_shapes=[
             *[dma((n_col - 1, LEFT_CUTS))] * 4,
             *[dma((n_chip - 1, RIGHT_CUTS))] * 2,
@@ -285,34 +283,39 @@
             *[dma((n_chip - 1, RIGHT_CUTS))] * 2,
             *[dma((n_col - 1,))] * 2,
             *[dma((n_row - 1,))] * 2,
+            *[dma] * 2,
         ],
-        compiler_params=pltpu.CompilerParams(collective_id=0, has_side_effects=True),
+        compiler_params=pltpu.CompilerParams(
+            collective_id=0, has_side_effects=True, vmem_limit_bytes=limit
+        ),
         name="gather_panels",
-    )(left, right, left_meta, right_meta)
+    )(left, right, meta)
     left_all, right_all, left_meta_all, right_meta_all = gathered
     kb_cols = n_row * sets * per // n_col
     blocks = GR * kb_cols
-    room = per * ma * mb + UNROLL
     out = pl.pallas_call(
         functools.partial(product_kernel, (n_row, n_col, sets, per, ma, mb, kb_cols)),
         out_shape=jax.ShapeDtypeStruct((blocks, 2 * width, width), jnp.bfloat16),
-        in_specs=[any_space] * 4 + [smem] * 2,
+        in_specs=[vmem] * 2 + [smem] * 2,
         out_specs=any_space,
         scratch_shapes=[
-            pltpu.VMEM((n_col, per * ma, 2 * width, width), left.dtype),
-            pltpu.VMEM((n_col, per * mb, 2 * width, width), right.dtype),
             pltpu.VMEM((blocks + 1, 2 * width, width), jnp.float32),
             pltpu.VMEM((blocks, 2 * width, width), jnp.bfloat16),
-            pltpu.SMEM((n_col * room,), jnp.int32),
-            pltpu.SMEM((n_col,), jnp.int32),
+            pltpu.SMEM((n_col * per * ma * mb + UNROLL,), jnp.int32),
             pltpu.SMEM((blocks + 1,), jnp.int32),
-            dma((n_col,)),
-            dma((n_col,)),
             dma((GR,)),
         ],
-        compiler_params=pltpu.CompilerParams(vmem_limit_bytes=60 * 1024 * 1024),
+        compiler_params=pltpu.CompilerParams(vmem_limit_bytes=limit),
         name="pair_products",
-    )(left, right, left_all, right_all, left_meta_all, right_meta_all)
+    )(
+        pltpu.with_memory_space_constraint(
+            left_all.reshape((-1,) + left.shape[1:]), pltpu.VMEM
+        ),
+        pltpu.with_memory_space_constraint(
+            right_all.reshape((-1,) + right.shape[2:]), pltpu.VMEM
+        ),
+        left_meta_all, right_meta_all,
+    )
     return out.reshape(GR, kb_cols, 2, width, width)
 
 

time: 171 us -> 163 us (0.953)
  local copies, waits for them, and re-layouts: 5.58 us -> 0.16 us
  Pallas kernels: 163 us -> 159 us
  other arithmetic: 0.76 us -> 2.75 us
    pallas_call x1, Pallas kernels: 19.8 us -> 15 us  [body(): pl.pallas_call(functools.partial(product_kernel, (n_row, n_col, sets, per...]
    unnamed x4 -> x0, local copies, waits for them, and re-layouts: 3.04 us -> none
where the time goes in v2:
time: 163 us; the launch traced here: 162 us
  Pallas kernels  159 us (98%)
  other arithmetic  2.75 us (2%)
    pallas_call x1, Pallas kernels, body(): pl.pallas_call(functools.partial(gather_kernel, n_row, n_col), out_shape=...  144 us
    pallas_call x1, Pallas kernels, body(): pl.pallas_call(functools.partial(product_kernel, (n_row, n_col, sets, per...  15 us

profile of v2, /device:TPU:0, one launch (start us, length us, event | category | flops | bytes accessed | tf_op | source)
XLA Modules:
  0.0 161.6 jit_solution(12855315076120624910)
XLA Ops:
  0.0 0.7 pad_add_fusion.1
  0.7 0.7 add_bitcast_fusion
  1.4 0.1 copy.13
  1.5 0.1 copy.12
  1.6 1.3 pad_add_fusion.meta
  2.9 143.7 %gather_panels.1 = (bf16[4,32,256,128]{3,2,1,0:T(8,128)(2,1)S(1)}, bf16[1,4,64,256,128]{4,3,2,1,0:T(8,128)(2,1)S(1)}, s32[4,24,128]{2,1,0:T(8,128)}, s32[4,24,128]{2,1,0:T(8,128)}) custom-call(bf16[32,256,128]{2,1,0:T(8,128)(2,1)} %bitcast.13, bf16[1,64,256,128]{3,2,1,0:T(8,128)(2,1)} %bitcast.12, s32[24,128]{1,0:T(8,128)} %pad_add_fusion.meta), custom_call_target="tpu_custom_call" | custom-call | tf_op jit(solution)/shard_map/gather_panels/pallas_call | solution.py:269
  146.6 15.0 %pair_products.1 = bf16[128,256,128]{2,1,0:T(8,128)(2,1)} custom-call(bf16[128,256,128]{2,1,0:T(8,128)(2,1)S(1)} %bitcast.11, bf16[256,256,128]{2,1,0:T(8,128)(2,1)S(1)} %bitcast.10, s32[4,24,128]{2,1,0:T(8,128)} %get-tuple-element.11.left_meta, s32[4,24,128]{2,1,0:T(8,128)} %get-tuple-element.12.right_meta), custom_call_target="tpu_custom_call" | custom-call | tf_op jit(solution)/shard_map/pair_products/pallas_call | solution.py:296
